TPU v7x, 32 devices: a whole 2x2x4 slice. The times are simulated.
32 devices in a mesh: member: 8 (over z, y), band: 4 (over x, core).
Axes of the slice: x: 2, y: 2, z: 4, core: 2. Of those that a mesh axis runs over, the one named last changes fastest.
Arguments:
- spectral: float32 [128, 768, 768], P('member', 'band'), parts along dimension 0, may hold values from -6 to 6
- coupling: float32 [8192, 1024], P(('member', 'band')), parts along dimension 0, may hold values from 0.02 to 162, as said below
- quadratic: float32 [8192, 1024], P(('member', 'band')), parts along dimension 0, may hold values from -1.5 to 1.5
Outputs:
- tendency_spectral: float32 [128, 768, 768], P('member', 'band'), parts along dimension 0
There are 8 independent parts, one for each index of `member`. A program takes and returns all parts, laid end to end along the dimension named above; each array names one. Nothing has to cross between parts.
Inputs may be any that keep to these rules, and one draw needn't show every extreme that they name: `coupling`: positive.
All inputs are finite; a program needn't handle non-finite values.
Results may differ from a plain program's by a relative error of at most 0.00008.
Values sent between devices are 32-bit elements; how exact they have to be, the bound alone decides.
A program may use at most 128 MiB of HBM per device.

v0:
```python
import math
import jax
import jax.numpy as jnp
from jax import lax
from jax.sharding import PartitionSpec as P


def tables(cells, coeffs):
    half_count = coeffs // 2
    position = jnp.arange(cells, dtype=jnp.int32)
    column = jnp.arange(coeffs, dtype=jnp.int32)
    wavenumber = jnp.where(column < half_count, column, column - half_count)
    turns = position[:, None] * wavenumber[None, :] % cells
    angles = turns.astype(jnp.float32) * (2.0 * math.pi / cells)
    basis_table = jnp.where(column[None, :] < half_count, jnp.cos(angles), jnp.sin(angles))
    synthesis = basis_table / math.sqrt(half_count)
    factor = jnp.where(wavenumber == 0, 1.0, 2.0) * (math.sqrt(half_count) / cells)
    analysis = (basis_table * factor[None, :]).T
    return (synthesis, analysis)


def on_device(spectral, coupling, quadratic):
    high = lax.Precision.HIGHEST
    coeffs = spectral.shape[2]
    cells = coupling.shape[1]
    synthesis, analysis = tables(cells, coeffs)
    points = float(cells * cells)
    section = jnp.einsum("lab,yb->lay", spectral, synthesis, precision=high)
    turned = lax.all_to_all(section, "band", split_axis=2, concat_axis=1, tiled=True)
    grid = jnp.einsum("xa,lay->lyx", synthesis, turned, precision=high)
    product = coupling[None] * grid
    product, local_sum = (product, jnp.sum(product * product, axis=(1, 2)))
    total = lax.psum(local_sum, "band")
    scaled = product / jnp.sqrt(total / points + 1e-06)[:, None, None]
    tendency = scaled + quadratic[None] * scaled * scaled
    back = jnp.einsum("ax,lyx->lya", analysis, tendency, precision=high)
    returned = lax.all_to_all(back, "band", split_axis=2, concat_axis=1, tiled=True)
    return jnp.einsum("by,lya->lab", analysis, returned, precision=high)


def solution(mesh):
    placed = (P("member", "band", None), P(("member", "band"), None), P(("member", "band"), None))
    return jax.shard_map(
        on_device, mesh=mesh, in_specs=placed, out_specs=P("member", "band", None), check_vma=False
    )
```

profile of v0, /device:TPU:0, one launch (start us, length us, event | category | flops | bytes accessed | tf_op | source)
XLA Modules:
  0.0 669.1 jit_solution(13568946825027268618)
XLA Ops:
  0.0 12.7 %fusion.59 = f32[1024,768,1]{1,0,2:T(8,128)S(1)} fusion(s32[768]{0:T(1024)S(1)} %add_select_fusion.1, pred[768]{0:T(1024)(128)(4,1)S(1)} %iota_compare_fusion), kind=kLoop, calls=%fused_computation.20.clone.1 | loop fusion | flops 12582912 | bytes 3149568 | tf_op jit(solution)/shard_map/lab,yb->lay/dot_general | solution.py:28
  12.7 34.2 %convolution_bitcast_fusion = f32[16,192,1024]{2,1,0:T(8,128)} fusion(f32[16,192,768]{2,1,0:T(8,128)} %param.3, f32[1024,768,1]{1,0,2:T(8,128)S(1)} %fusion.59), kind=kOutput, calls=%fused_computation.11 | convolution fusion | flops 28991029248 | bytes 25165824 | tf_op jit(solution)/shard_map/lab,yb->lay/dot_general | solution.py:28
  46.9 17.7 %copy.15 = f32[16,192,1024]{1,0,2:T(8,128)} copy(f32[16,192,1024]{2,1,0:T(8,128)} %convolution_bitcast_fusion) | data formatting | bytes 25165824 | tf_op jit(solution)/shard_map/lab,yb->lay/dot_general | solution.py:28
  64.6 18.3 %all-to-all-start = ((f32[16,192,1024]{1,0,2:T(8,128)}), f32[16,192,1024]{1,0,2:T(8,128)}, u32[]{:S(2)}, u32[]{:S(2)}) async-start(f32[16,192,1024]{1,0,2:T(8,128)} %copy.15), calls=%async_computation | async-start | bytes 33554432 | tf_op jit(solution)/shard_map/all_to_all | solution.py:29
  83.0 12.4 %fusion.13.clone.4 = f32[1024,768,1]{1,0,2:T(8,128)S(1)} fusion(s32[768]{0:T(1024)S(1)} %add_select_fusion.1, pred[768]{0:T(1024)(128)(4,1)S(1)} %iota_compare_fusion), kind=kLoop, calls=%fused_computation.19.clone.clone.clone.1 | loop fusion | flops 12582912 | bytes 3149568 | tf_op jit(solution)/shard_map/reduce_sum | solution.py:32
  95.4 159.9 %all-to-all-done = f32[16,192,1024]{1,0,2:T(8,128)} async-done(((f32[16,192,1024]{1,0,2:T(8,128)}), f32[16,192,1024]{1,0,2:T(8,128)}, u32[]{:S(2)}, u32[]{:S(2)}) %all-to-all-start) | async-done | bytes 12582944 | tf_op jit(solution)/shard_map/all_to_all | solution.py:29
  255.3 14.5 %copy.23 = f32[16,192,4,256]{3,2,1,0:T(4,128)} copy(f32[16,192,4,256]{1,0,3,2:T(8,128)} %bitcast.2) | data formatting | bytes 25165824 | tf_op jit(solution)/shard_map/all_to_all | solution.py:29
  269.8 0.0 copy-start
  269.8 11.3 %copy.17 = f32[16,4,192,256]{3,2,1,0:T(8,128)} copy(f32[16,4,192,256]{3,1,2,0:T(4,128)} %bitcast.45) | data formatting | bytes 25165824 | tf_op jit(solution)/shard_map/all_to_all | solution.py:29
  281.1 0.0 copy-done
  281.1 83.8 %multiply_reduce_fusion = (f32[16]{0:T(128)S(1)}, f32[16,256,1024]{2,1,0:T(8,128)}) fusion(f32[256,1024]{1,0:T(8,128)S(1)} %copy-done, f32[16,768,256]{2,1,0:T(8,128)} %bitcast.46, f32[1024,768,1]{1,0,2:T(8,128)S(1)} %fusion.13.clone.4), kind=kOutput, calls=%fused_computation.3 | convolution fusion | flops 38667288576 | bytes 33554496 | tf_op jit(solution)/shard_map/xa,lay->lyx/dot_general | solution.py:30
  365.0 5.8 psum.7
  370.7 12.9 %multiply_add_fusion.5 = f32[16,256,1024]{2,1,0:T(8,128)} fusion(f32[16,256,1024]{2,1,0:T(8,128)} %get-tuple-element.6, f32[256,1024]{1,0:T(8,128)} %param.5, f32[16]{0:T(128)S(1)} %add_sqrt_fusion, f32[256,1024]{1,0:T(8,128)} %param.4), kind=kLoop, calls=%fused_computation.clone.clone.2 | loop fusion | flops 20971520 | bytes 35651648 | tf_op jit(solution)/shard_map/ax,lyx->lya/dot_general | solution.py:36
  383.7 58.5 %fusion = f32[16,256,768]{2,1,0:T(8,128)} fusion(f32[768]{0:T(1024)S(1)} %select_multiply_fusion, s32[768]{0:T(1024)S(1)} %add_select_fusion.1, pred[768]{0:T(1024)(128)(4,1)S(1)} %iota_compare_fusion, f32[16,256,1024]{2,1,0:T(8,128)} %multiply_add_fusion.5), kind=kOutput, calls=%fused_computation.1 | convolution fusion | flops 38667288576 | bytes 29367040 | tf_op jit(solution)/shard_map/ax,lyx->lya/dot_general | solution.py:36
  442.2 12.8 %copy.19 = f32[16,256,768]{1,0,2:T(8,128)} copy(f32[16,256,768]{2,1,0:T(8,128)} %fusion) | data formatting | bytes 25165824 | tf_op jit(solution)/shard_map/ax,lyx->lya/dot_general | solution.py:36
  455.0 6.5 all-to-all-start.1
  461.5 12.7 %fusion.61 = f32[1024,768,1]{1,0,2:T(8,128)S(1)} fusion(f32[768]{0:T(1024)S(1)} %select_multiply_fusion, s32[768]{0:T(1024)S(1)} %add_select_fusion.1, pred[768]{0:T(1024)(128)(4,1)S(1)} %iota_compare_fusion), kind=kLoop, calls=%fused_computation.16.clone.1 | loop fusion | flops 12582912 | bytes 3152640 | tf_op jit(solution)/shard_map/by,lya->lab/dot_general | solution.py:38
  474.2 125.2 %all-to-all-done.1 = f32[16,256,768]{1,0,2:T(8,128)} async-done(((f32[16,256,768]{1,0,2:T(8,128)}), f32[16,256,768]{1,0,2:T(8,128)}, u32[]{:S(2)}, u32[]{:S(2)}) %all-to-all-start.1) | async-done | bytes 12582944 | tf_op jit(solution)/shard_map/all_to_all | solution.py:37
  599.4 16.5 %copy.21 = f32[16,4,256,192]{2,1,3,0:T(4,128)} copy(f32[16,4,256,192]{2,0,3,1:T(8,128)} %bitcast.8) | data formatting | bytes 25165824 | tf_op jit(solution)/shard_map/all_to_all | solution.py:37
  615.9 15.7 %all_to_all.33 = f32[16,1024,192]{1,2,0:T(8,128)} reshape(f32[16,4,256,192]{2,1,3,0:T(4,128)} %copy.21) | data formatting | bytes 25165824 | tf_op jit(solution)/shard_map/all_to_all | solution.py:37
  631.6 37.1 %fusion.9 = f32[16,192,768]{2,1,0:T(8,128)} fusion(f32[16,1024,192]{1,2,0:T(8,128)} %all_to_all.33, f32[1024,768,1]{1,0,2:T(8,128)S(1)} %fusion.61), kind=kOutput, calls=%fused_computation.15 | convolution fusion | flops 28991029248 | bytes 25165824 | tf_op jit(solution)/shard_map/by,lya->lab/dot_general | solution.py:38
  (4 shorter events, 0.0 us)
Async XLA Ops:
  64.6 190.7 %all-to-all-start = ((f32[16,192,1024]{1,0,2:T(8,128)}), f32[16,192,1024]{1,0,2:T(8,128)}, u32[]{:S(2)}, u32[]{:S(2)}) async-start(f32[16,192,1024]{1,0,2:T(8,128)} %copy.15), calls=%async_computation | async-start | bytes 33554432 | tf_op jit(solution)/shard_map/all_to_all | solution.py:29
  269.8 11.3 %copy-start = (f32[256,1024]{1,0:T(8,128)S(1)}, f32[256,1024]{1,0:T(8,128)}, u32[]{:S(2)}) copy-start(f32[256,1024]{1,0:T(8,128)} %param.4) | copy-start | bytes 3145732
  455.0 144.4 %all-to-all-start.1 = ((f32[16,256,768]{1,0,2:T(8,128)}), f32[16,256,768]{1,0,2:T(8,128)}, u32[]{:S(2)}, u32[]{:S(2)}) async-start(f32[16,256,768]{1,0,2:T(8,128)} %copy.19), calls=%async_computation.1 | async-start | bytes 25165824 | tf_op jit(solution)/shard_map/all_to_all | solution.py:37
where the time goes:
time: 679 us; the launch traced here: 669 us
  waiting for transfers between devices  285 us (42%)
  matrix products  214 us (32%)
  local copies, waits for them, and re-layouts  88.5 us (13%)
  other arithmetic  50.8 us (7%)
  starting transfers between devices  24.9 us (4%)
    all_to_all x1, waiting for transfers between devices, on_device(): lax.all_to_all(section, 'band', split_axis=2, concat_axis=1, tiled=True)  160 us
    all_to_all x1, waiting for transfers between devices, on_device(): lax.all_to_all(back, 'band', split_axis=2, concat_axis=1, tiled=True)  125 us
    dot_general x1, matrix products, on_device(): grid = jnp.einsum('xa,lay->lyx', synthesis, turned, precision=high)  83.8 us
    dot_general x1, matrix products, on_device(): back = jnp.einsum('ax,lyx->lya', analysis, tendency, precision=high)  58.5 us
    dot_general x1, matrix products, on_device(): return jnp.einsum('by,lya->lab', analysis, returned, precision=high)  37.1 us
    dot_general x1, matrix products, on_device(): section = jnp.einsum('lab,yb->lay', spectral, synthesis, precision=high)  34.2 us
    all_to_all x2, local copies, waits for them, and re-layouts, on_device(): lax.all_to_all(back, 'band', split_axis=2, concat_axis=1, tiled=True)  32.2 us
    all_to_all x2, local copies, waits for them, and re-layouts, on_device(): lax.all_to_all(section, 'band', split_axis=2, concat_axis=1, tiled=True)  25.8 us
  transfers between devices with their start and end apart: 2, of which 2 were waited for; matrix products, arithmetic and copies ran while one was open for 4% of the time, Pallas kernels for 0%

commit v1 on v0

--- a/solution.py
+++ b/solution.py
@@ -26,7 +26,12 @@
     synthesis, analysis = tables(cells, coeffs)
     points = float(cells * cells)
     section = jnp.einsum("lab,yb->lay", spectral, synthesis, precision=high)
-    turned = lax.all_to_all(section, "band", split_axis=2, concat_axis=1, tiled=True)
+    turned = jnp.concatenate(
+        lax.all_to_all(
+            jnp.stack(jnp.split(section, lax.axis_size("band"), axis=2), axis=0), "band", 0, 0
+        ),
+        axis=1,
+    )
     grid = jnp.einsum("xa,lay->lyx", synthesis, turned, precision=high)
     product = coupling[None] * grid
     product, local_sum = (product, jnp.sum(product * product, axis=(1, 2)))

time: 679 us -> 617 us (0.909)
  waiting for transfers between devices: 285 us -> 241 us
  local copies, waits for them, and re-layouts: 88.5 us -> 64.7 us
  other arithmetic: 50.8 us -> 58.5 us
    all_to_all x1, waiting for transfers between devices: 160 us -> 116 us  [on_device(): lax.all_to_all(jnp.stack(jnp.split(section, lax.axis_size('band'), axis=2...]
    all_to_all x2 -> x0, local copies, waits for them, and re-layouts: 25.8 us -> none  [on_device(): lax.all_to_all(section, 'band', split_axis=2, concat_axis=1, tiled=True)]
    dot_general x1 -> x0, local copies, waits for them, and re-layouts: 17.7 us -> none  [on_device(): section = jnp.einsum('lab,yb->lay', spectral, synthesis, precision=high)]
    reshape x0 -> x1, local copies, waits for them, and re-layouts: none -> 10.7 us  [on_device(): jnp.concatenate(lax.all_to_all(jnp.stack(jnp.split(section, lax.axis_size...]
    another operation x0 -> x1, local copies, waits for them, and re-layouts: none -> 9 us  [on_device(): jnp.stack(jnp.split(section, lax.axis_size('band'), axis=2), axis=0)]
    another operation x0 -> x1, other arithmetic: none -> 7.79 us  [on_device(): jnp.stack(jnp.split(section, lax.axis_size('band'), axis=2), axis=0)]
where the time goes in v1:
time: 617 us; the launch traced here: 607 us
  waiting for transfers between devices  241 us (39%)
  matrix products  214 us (35%)
  local copies, waits for them, and re-layouts  64.7 us (10%)
  other arithmetic  58.5 us (9%)
  starting transfers between devices  22.9 us (4%)
    all_to_all x1, waiting for transfers between devices, on_device(): lax.all_to_all(back, 'band', split_axis=2, concat_axis=1, tiled=True)  125 us
    all_to_all x1, waiting for transfers between devices, on_device(): lax.all_to_all(jnp.stack(jnp.split(section, lax.axis_size('band'), axis=2...  116 us
    dot_general x1, matrix products, on_device(): grid = jnp.einsum('xa,lay->lyx', synthesis, turned, precision=high)  83.8 us
    dot_general x1, matrix products, on_device(): back = jnp.einsum('ax,lyx->lya', analysis, tendency, precision=high)  58.6 us
    dot_general x1, matrix products, on_device(): return jnp.einsum('by,lya->lab', analysis, returned, precision=high)  37.1 us
    dot_general x1, matrix products, on_device(): section = jnp.einsum('lab,yb->lay', spectral, synthesis, precision=high)  34.2 us
    all_to_all x2, local copies, waits for them, and re-layouts, on_device(): lax.all_to_all(back, 'band', split_axis=2, concat_axis=1, tiled=True)  32.2 us
    all_to_all x1, starting transfers between devices, on_device(): lax.all_to_all(jnp.stack(jnp.split(section, lax.axis_size('band'), axis=2...  16.3 us
  transfers between devices with their start and end apart: 2, of which 2 were waited for; matrix products, arithmetic and copies ran while one was open for 4% of the time, Pallas kernels for 0%

profile of v1, /device:TPU:0, one launch (start us, length us, event | category | flops | bytes accessed | tf_op | source)
XLA Modules:
  0.0 607.5 jit_solution(4162077328491786197)
XLA Ops:
  0.0 12.7 %fusion.59 = f32[1024,768,1]{1,0,2:T(8,128)S(1)} fusion(s32[768]{0:T(1024)S(1)} %add_select_fusion.1, pred[768]{0:T(1024)(128)(4,1)S(1)} %iota_compare_fusion), kind=kLoop, calls=%fused_computation.25.clone.1 | loop fusion | flops 12582912 | bytes 3149568 | tf_op jit(solution)/shard_map/lab,yb->lay/dot_general | solution.py:28
  12.7 34.2 %convolution_bitcast_fusion = f32[16,192,1024]{2,1,0:T(8,128)} fusion(f32[16,192,768]{2,1,0:T(8,128)} %param.3, f32[1024,768,1]{1,0,2:T(8,128)S(1)} %fusion.59), kind=kOutput, calls=%fused_computation.12 | convolution fusion | flops 28991029248 | bytes 25165824 | tf_op jit(solution)/shard_map/lab,yb->lay/dot_general | solution.py:28
  46.9 9.0 %slice_bitcast_fusion.3 = (f32[1,16,192,256]{3,2,1,0:T(8,128)S(1)}, f32[1,16,192,256]{3,2,1,0:T(8,128)S(1)}, f32[1,16,192,256]{3,2,1,0:T(8,128)}, f32[1,16,192,256]{3,2,1,0:T(8,128)}) fusion(f32[16,192,1024]{2,1,0:T(8,128)} %convolution_bitcast_fusion), kind=kLoop, calls=%fused_computation.19 | loop fusion | bytes 25165824 | tf_op jit(solution)/shard_map/stack | solution.py:31
  55.9 7.8 %pad_maximum_fusion = f32[4,16,192,256]{3,2,1,0:T(8,128)} fusion(f32[1,16,192,256]{3,2,1,0:T(8,128)S(1)} %get-tuple-element.6, f32[1,16,192,256]{3,2,1,0:T(8,128)} %get-tuple-element.7, f32[1,16,192,256]{3,2,1,0:T(8,128)} %get-tuple-element.8, f32[1,16,192,256]{3,2,1,0:T(8,128)S(1)} %get-tuple-element.5), kind=kLoop, calls=%fused_computation.5 | loop fusion | flops 9437184 | bytes 25165824 | tf_op jit(solution)/shard_map/stack | solution.py:31
  63.7 16.3 %all-to-all-start = ((f32[4,16,192,256]{3,2,1,0:T(8,128)}), f32[4,16,192,256]{3,2,1,0:T(8,128)}, u32[]{:S(2)}, u32[]{:S(2)}) async-start(f32[4,16,192,256]{3,2,1,0:T(8,128)} %pad_maximum_fusion), calls=%async_computation | async-start | bytes 25165824 | tf_op jit(solution)/shard_map/all_to_all | solution.py:30
  80.1 12.4 %fusion.13.clone.4 = f32[1024,768,1]{1,0,2:T(8,128)S(1)} fusion(s32[768]{0:T(1024)S(1)} %add_select_fusion.1, pred[768]{0:T(1024)(128)(4,1)S(1)} %iota_compare_fusion), kind=kLoop, calls=%fused_computation.24.clone.clone.clone.1 | loop fusion | flops 12582912 | bytes 3149568 | tf_op jit(solution)/shard_map/reduce_sum | solution.py:37
  92.5 116.3 %all-to-all-done = f32[4,16,192,256]{3,2,1,0:T(8,128)} async-done(((f32[4,16,192,256]{3,2,1,0:T(8,128)}), f32[4,16,192,256]{3,2,1,0:T(8,128)}, u32[]{:S(2)}, u32[]{:S(2)}) %all-to-all-start) | async-done | bytes 12582944 | tf_op jit(solution)/shard_map/all_to_all | solution.py:30
  208.8 0.0 copy-start
  208.8 10.7 %copy.9 = f32[16,4,192,256]{3,2,1,0:T(8,128)} copy(f32[16,4,192,256]{3,2,0,1:T(8,128)} %bitcast.6) | data formatting | bytes 25165824 | tf_op jit(solution)/shard_map/reshape | solution.py:29
  219.5 0.0 copy-done
  219.5 83.8 %multiply_reduce_fusion = (f32[16]{0:T(128)S(1)}, f32[16,256,1024]{2,1,0:T(8,128)}) fusion(f32[256,1024]{1,0:T(8,128)S(1)} %copy-done, f32[16,768,256]{2,1,0:T(8,128)} %bitcast.52, f32[1024,768,1]{1,0,2:T(8,128)S(1)} %fusion.13.clone.4), kind=kOutput, calls=%fused_computation.3 | convolution fusion | flops 38667288576 | bytes 33554496 | tf_op jit(solution)/shard_map/xa,lay->lyx/dot_general | solution.py:35
  303.3 5.8 psum.7
  309.1 12.9 %multiply_add_fusion.5 = f32[16,256,1024]{2,1,0:T(8,128)} fusion(f32[16,256,1024]{2,1,0:T(8,128)} %get-tuple-element.10, f32[256,1024]{1,0:T(8,128)} %param.5, f32[16]{0:T(128)S(1)} %add_sqrt_fusion, f32[256,1024]{1,0:T(8,128)} %param.4), kind=kLoop, calls=%fused_computation.clone.clone.2 | loop fusion | flops 20971520 | bytes 35651648 | tf_op jit(solution)/shard_map/ax,lyx->lya/dot_general | solution.py:41
  322.0 58.6 %fusion = f32[16,256,768]{2,1,0:T(8,128)} fusion(f32[768]{0:T(1024)S(1)} %select_multiply_fusion, s32[768]{0:T(1024)S(1)} %add_select_fusion.1, pred[768]{0:T(1024)(128)(4,1)S(1)} %iota_compare_fusion, f32[16,256,1024]{2,1,0:T(8,128)} %multiply_add_fusion.5), kind=kOutput, calls=%fused_computation.1 | convolution fusion | flops 38667288576 | bytes 29367040 | tf_op jit(solution)/shard_map/ax,lyx->lya/dot_general | solution.py:41
  380.6 12.8 %copy.11 = f32[16,256,768]{1,0,2:T(8,128)} copy(f32[16,256,768]{2,1,0:T(8,128)} %fusion) | data formatting | bytes 25165824 | tf_op jit(solution)/shard_map/ax,lyx->lya/dot_general | solution.py:41
  393.4 6.5 %all-to-all-start.1 = ((f32[16,256,768]{1,0,2:T(8,128)}), f32[16,256,768]{1,0,2:T(8,128)}, u32[]{:S(2)}, u32[]{:S(2)}) async-start(f32[16,256,768]{1,0,2:T(8,128)} %copy.11), calls=%async_computation.1 | async-start | bytes 25165824 | tf_op jit(solution)/shard_map/all_to_all | solution.py:42
  399.9 12.7 %fusion.61 = f32[1024,768,1]{1,0,2:T(8,128)S(1)} fusion(f32[768]{0:T(1024)S(1)} %select_multiply_fusion, s32[768]{0:T(1024)S(1)} %add_select_fusion.1, pred[768]{0:T(1024)(128)(4,1)S(1)} %iota_compare_fusion), kind=kLoop, calls=%fused_computation.21.clone.1 | loop fusion | flops 12582912 | bytes 3152640 | tf_op jit(solution)/shard_map/by,lya->lab/dot_general | solution.py:43
  412.6 125.2 %all-to-all-done.1 = f32[16,256,768]{1,0,2:T(8,128)} async-done(((f32[16,256,768]{1,0,2:T(8,128)}), f32[16,256,768]{1,0,2:T(8,128)}, u32[]{:S(2)}, u32[]{:S(2)}) %all-to-all-start.1) | async-done | bytes 12582944 | tf_op jit(solution)/shard_map/all_to_all | solution.py:42
  537.8 16.5 %copy.13 = f32[16,4,256,192]{2,1,3,0:T(4,128)} copy(f32[16,4,256,192]{2,0,3,1:T(8,128)} %bitcast.11) | data formatting | bytes 25165824 | tf_op jit(solution)/shard_map/all_to_all | solution.py:42
  554.3 15.7 %all_to_all.20 = f32[16,1024,192]{1,2,0:T(8,128)} reshape(f32[16,4,256,192]{2,1,3,0:T(4,128)} %copy.13) | data formatting | bytes 25165824 | tf_op jit(solution)/shard_map/all_to_all | solution.py:42
  569.9 37.1 %fusion.9 = f32[16,192,768]{2,1,0:T(8,128)} fusion(f32[16,1024,192]{1,2,0:T(8,128)} %all_to_all.20, f32[1024,768,1]{1,0,2:T(8,128)S(1)} %fusion.61), kind=kOutput, calls=%fused_computation.20 | convolution fusion | flops 28991029248 | bytes 25165824 | tf_op jit(solution)/shard_map/by,lya->lab/dot_general | solution.py:43
  (4 shorter events, 0.0 us)
Async XLA Ops:
  63.7 145.1 %all-to-all-start = ((f32[4,16,192,256]{3,2,1,0:T(8,128)}), f32[4,16,192,256]{3,2,1,0:T(8,128)}, u32[]{:S(2)}, u32[]{:S(2)}) async-start(f32[4,16,192,256]{3,2,1,0:T(8,128)} %pad_maximum_fusion), calls=%async_computation | async-start | bytes 25165824 | tf_op jit(solution)/shard_map/all_to_all | solution.py:30
  208.8 10.7 %copy-start = (f32[256,1024]{1,0:T(8,128)S(1)}, f32[256,1024]{1,0:T(8,128)}, u32[]{:S(2)}) copy-start(f32[256,1024]{1,0:T(8,128)} %param.4) | copy-start | bytes 3145732
  393.4 144.4 %all-to-all-start.1 = ((f32[16,256,768]{1,0,2:T(8,128)}), f32[16,256,768]{1,0,2:T(8,128)}, u32[]{:S(2)}, u32[]{:S(2)}) async-start(f32[16,256,768]{1,0,2:T(8,128)} %copy.11), calls=%async_computation.1 | async-start | bytes 25165824 | tf_op jit(solution)/shard_map/all_to_all | solution.py:42
